TPU v7x, 32 devices: a whole 2x2x4 slice. The times are simulated.
32 devices in a mesh: rows: 4 (over y, x), batch: 8 (over z, core).
Axes of the slice: x: 2, y: 2, z: 4, core: 2. Of those that a mesh axis runs over, the one named last changes fastest.
Arguments:
- control: bfloat16 [8, 24, 96, 320], P('batch', 'rows'), may hold values from -60 to 60, as said below
- unet_skips: bfloat16 [2, 8, 24, 96, 320], P(None, 'batch', 'rows'), may hold values from -6 to 6
- norm_gains: float32 [2, 2, 320], replicated, may hold values from 0.25 to 1.75
- norm_shifts: float32 [2, 2, 320], replicated, may hold values from -3 to 3
- conv_weights: bfloat16 [2, 2, 3, 960, 320], P(None, None, None, None, 'batch'), may hold values from -0.109375 to 0.109375
- zero_weights: bfloat16 [2, 1, 320, 320], P(None, None, None, 'batch'), may hold values from -0.3125 to 0.3125
Outputs:
- controls: bfloat16 [2, 8, 24, 96, 320], P(None, 'batch', 'rows')
Inputs may be any that keep to these rules, and one draw needn't show every extreme that they name: `control`: Real-valued latent features.
All inputs are finite; a program needn't handle non-finite values.
Results may differ from a plain program's by a relative error of at most 0.01.
Values may be sent and summed in bfloat16 or wider, within the bound.
A program may use at most 64 MiB of HBM per device.

v0:
```python
import jax
import jax.numpy as jnp
from jax import lax
from jax.sharding import PartitionSpec as P

GROUPS = 32
epsilon = 1e-05


def extended(block, sides, width):
    for axis, dim in sides:
        count = lax.axis_size(axis)
        forward = [(i, i + 1) for i in range(count - 1)]
        backward = [(target, source) for source, target in forward]
        low = lax.ppermute(
            lax.slice_in_dim(block, block.shape[dim] - width, None, axis=dim), axis, forward
        )
        high = lax.ppermute(lax.slice_in_dim(block, 0, width, axis=dim), axis, backward)
        block = jnp.concatenate([low, block, high], axis=dim)
    return block


def normalize(values, gain_row, shift_row):
    samples, height, across, channels = values.shape
    members = height * lax.axis_size("rows") * across * (channels // GROUPS)
    grouped = values.astype(jnp.float32).reshape(
        samples, height, across, GROUPS, channels // GROUPS
    )
    partial_sum, partial_square = lax.psum(
        (
            jnp.sum(grouped, axis=(1, 2, 4), keepdims=True),
            jnp.sum(grouped * grouped, axis=(1, 2, 4), keepdims=True),
        ),
        "rows",
    )
    average = partial_sum / members
    spread = partial_square / members - average * average
    centered = grouped - average
    scaled = (centered * lax.rsqrt(spread + epsilon)).reshape(
        samples, height, across, channels
    ) * gain_row + shift_row
    return jax.nn.silu(scaled).astype(jnp.bfloat16)


def apply_taps(padded, weight_piece):
    tap_rows = weight_piece.shape[0]
    tap_cols = weight_piece.shape[1] // padded.shape[3]
    height = padded.shape[1] - tap_rows + 1
    across = padded.shape[2] - tap_cols + 1
    summed = jnp.zeros((padded.shape[0], height, across, weight_piece.shape[2]), jnp.float32)
    for row_tap in range(tap_rows):
        row_band = padded[:, row_tap : row_tap + height]
        if tap_cols > 1:
            stacked = jnp.concatenate(
                [row_band[:, :, col_tap : col_tap + across] for col_tap in range(tap_cols)], axis=3
            )
        else:
            stacked = row_band
        summed = summed + jnp.einsum(
            "bhwk,kc->bhwc", stacked, weight_piece[row_tap], preferred_element_type=jnp.float32
        )
    return summed


def convolve(values, weight):
    if weight.shape[0] > 1:
        padded = extended(values, (("rows", 1),), 1)
        padded = jnp.pad(padded, ((0, 0), (0, 0), (1, 1), (0, 0)))
    else:
        padded = values
    complete = lax.all_gather(weight, "batch", axis=2, tiled=True)
    return apply_taps(padded, complete)


def on_device(control, unet_skips, norm_gains, norm_shifts, conv_weights, zero_weights):
    hidden = control
    results = []
    for layer_index in range(conv_weights.shape[0]):
        normed = normalize(hidden, norm_gains[layer_index, 0], norm_shifts[layer_index, 0])
        first = convolve(normed, conv_weights[layer_index, 0]).astype(jnp.bfloat16)
        normed_two = normalize(first, norm_gains[layer_index, 1], norm_shifts[layer_index, 1])
        second = convolve(normed_two, conv_weights[layer_index, 1])
        hidden = (hidden.astype(jnp.float32) + second).astype(jnp.bfloat16)
        zeroed = convolve(hidden, zero_weights[layer_index])
        results.append((zeroed + unet_skips[layer_index].astype(jnp.float32)).astype(jnp.bfloat16))
    return jnp.stack(results)


def solution(mesh):
    placed = (
        P("batch", "rows", None, None),
        P(None, "batch", "rows", None, None),
        P(),
        P(),
        P(None, None, None, None, "batch"),
        P(None, None, None, "batch"),
    )
    return jax.shard_map(
        on_device,
        mesh=mesh,
        in_specs=placed,
        out_specs=P(None, "batch", "rows", None, None),
        check_vma=False,
    )
```

profile of v0, /device:TPU:0, one launch (start us, length us, event | category | flops | bytes accessed | tf_op | source)
XLA Modules:
  0.0 152.8 jit_solution(14512298526885135947)
XLA Ops:
  6.6 2.3 %fusion.153 = (bf16[1,1,3,960,40]{3,4,2,1,0:T(8,128)(2,1)}, bf16[1,1,3,960,40]{3,4,2,1,0:T(8,128)(2,1)}, bf16[1,1,3,960,40]{3,4,2,1,0:T(8,128)(2,1)}, bf16[1,1,3,960,40]{3,4,2,1,0:T(8,128)(2,1)}) fusion(bf16[2,2,3,960,40]{3,4,2,1,0:T(8,128)(2,1)} %param.10), kind=kLoop, calls=%fused_computation.215 | loop fusion | bytes 1843200 | tf_op jit(solution)/shard_map/slice | solution.py:82
  11.1 11.4 %all-reduce.7 = (f32[1,1,1,32,1]{3,4,2,1,0:T(1,128)S(1)}, f32[1,1,1,32,1]{3,4,2,1,0:T(1,128)S(1)}) all-reduce(f32[1,1,1,32,1]{3,4,2,1,0:T(1,128)S(1)} %bitcast.189, f32[1,1,1,32,1]{3,4,2,1,0:T(1,128)S(1)} %bitcast.187), channel_id=1, replica_groups=mesh['rows'=4,'batch'=8] {'rows'}, use_global_device_ids=true, to_apply=%region_5.6 | all-reduce | flops 64 | bytes 512 | tf_op jit(solution)/shard_map/psum | solution.py:29
  23.8 2.2 %collective-permute-start = (bf16[1,1,96,320]{3,2,1,0:T(8,128)(2,1)S(1)}, bf16[1,1,96,320]{3,2,1,0:T(8,128)(2,1)}, u32[]{:S(2)}, u32[]{:S(2)}) collective-permute-start(bf16[1,1,96,320]{3,2,1,0:T(8,128)(2,1)S(1)} %get-tuple-element.64), channel_id=1, source_target_pairs={{0,8},{8,16},{16,24},{1,9},{9,17},{17,25},{2,10},{10,18},{18,26},{... | collective-permute-start | bytes 184328 | tf_op jit(solution)/shard_map/ppermute | solution.py:15
  26.0 1.3 collective-permute-start.1
  28.0 4.3 %collective-permute-done.1 = bf16[1,1,96,320]{3,2,1,0:T(8,128)(2,1)S(1)} collective-permute-done((bf16[1,1,96,320]{3,2,1,0:T(8,128)(2,1)S(1)}, bf16[1,1,96,320]{3,2,1,0:T(8,128)(2,1)S(1)}, u32[]{:S(2)}, u32[]{:S(2)}) %collective-permute-start.1) | collective-permute-done | bytes 61472 | tf_op jit(solution)/shard_map/ppermute | solution.py:18
  32.9 1.1 fusion.134
  34.3 5.6 %all-gather.11.cloned.1.call-done = bf16[1,1,3,960,320]{3,4,2,1,0:T(8,128)(2,1)} async-done(((bf16[1,1,3,960,40]{3,4,2,1,0:T(8,128)(2,1)}), bf16[1,1,3,960,320]{3,4,2,1,0:T(8,128)(2,1)}) %all-gather.11.cloned.1.call-update) | async-done | bytes 1843216 | tf_op jit(solution)/shard_map/all_gather | solution.py:71
  39.9 2.0 %fusion.53 = f32[6,96,320]{2,1,0:T(8,128)S(1)} fusion(bf16[1,6,96,320]{3,2,1,0:T(8,128)(2,1)S(1)} %fusion.116, bf16[1,1,96,320]{3,2,1,0:T(8,128)(2,1)} %collective-permute-done, bf16[1,6,96,320]{3,2,1,0:T(8,128)(2,1)S(1)} %get-tuple-element.54, bf16[1,6,96,320]{3,2,1,0:T(8,128)(2,1)S(1)} %get-tuple-element.55, ...), kind=kOutput, calls=%fused_computation.80 | convolution fusion | flops 358318080 | bytes 2572288 | tf_op jit(solution)/shard_map/bhwk,kc->bhwc/dot_general | solution.py:59
  42.8 0.8 convert_reduce_fusion.3
  44.1 9.8 %all-reduce.6 = (f32[1,1,1,32,1]{3,4,2,1,0:T(1,128)S(1)}, f32[1,1,1,32,1]{3,4,2,1,0:T(1,128)S(1)}) all-reduce(f32[1,1,1,32,1]{3,4,2,1,0:T(1,128)S(1)} %bitcast.190, f32[1,1,1,32,1]{3,4,2,1,0:T(1,128)S(1)} %bitcast.185), channel_id=1, replica_groups=mesh['rows'=4,'batch'=8] {'rows'}, use_global_device_ids=true, to_apply=%region_11.12 | all-reduce | flops 64 | bytes 512 | tf_op jit(solution)/shard_map/psum | solution.py:29
  54.7 1.7 %collective-permute-start.2 = (bf16[1,1,96,320]{3,2,1,0:T(8,128)(2,1)S(1)}, bf16[1,1,96,320]{3,2,1,0:T(8,128)(2,1)S(1)}, u32[]{:S(2)}, u32[]{:S(2)}) collective-permute-start(bf16[1,1,96,320]{3,2,1,0:T(8,128)(2,1)S(1)} %get-tuple-element.62), channel_id=1, source_target_pairs={{0,8},{8,16},{16,24},{1,9},{9,17},{17,25},{2,10},{10,18},{18,26},{... | collective-permute-start | bytes 184328 | tf_op jit(solution)/shard_map/ppermute | solution.py:15
  56.4 1.3 collective-permute-start.3
  57.7 16.0 %all-gather.5 = bf16[1,1,320,320]{2,3,1,0:T(8,128)(2,1)} all-gather(bf16[1,1,320,40]{2,3,1,0:T(8,128)(2,1)S(1)} %copy-done.4), channel_id=7, replica_groups=mesh['rows'=4,'batch'=8] {'batch'}, dimensions={3}, use_global_device_ids=true | all-gather | bytes 230400 | tf_op jit(solution)/shard_map/all_gather | solution.py:71
  75.5 2.1 %fusion.42 = f32[6,96,320]{2,1,0:T(8,128)S(1)} fusion(bf16[1,6,96,320]{3,2,1,0:T(8,128)(2,1)S(1)} %fusion.136, bf16[1,1,96,320]{3,2,1,0:T(8,128)(2,1)} %copy-done.11, bf16[1,6,96,320]{3,2,1,0:T(8,128)(2,1)S(1)} %get-tuple-element.48, bf16[1,6,96,320]{3,2,1,0:T(8,128)(2,1)S(1)} %get-tuple-element.49, ...), kind=kOutput, calls=%fused_computation.69 | convolution fusion | flops 358318080 | bytes 2572288 | tf_op jit(solution)/shard_map/bhwk,kc->bhwc/dot_general | solution.py:59
  78.4 0.9 convert_reduce_fusion
  79.7 11.0 %all-reduce.5 = (f32[1,1,1,32,1]{3,4,2,1,0:T(1,128)S(1)}, f32[1,1,1,32,1]{3,4,2,1,0:T(1,128)S(1)}) all-reduce(f32[1,1,1,32,1]{3,4,2,1,0:T(1,128)S(1)} %bitcast.191, f32[1,1,1,32,1]{3,4,2,1,0:T(1,128)S(1)} %bitcast.186), channel_id=1, replica_groups=mesh['rows'=4,'batch'=8] {'rows'}, use_global_device_ids=true, to_apply=%region_17.18 | all-reduce | flops 64 | bytes 512 | tf_op jit(solution)/shard_map/psum | solution.py:29
  91.4 3.3 %collective-permute-start.4 = (bf16[1,1,96,320]{3,2,1,0:T(8,128)(2,1)S(1)}, bf16[1,1,96,320]{3,2,1,0:T(8,128)(2,1)S(1)}, u32[]{:S(2)}, u32[]{:S(2)}) collective-permute-start(bf16[1,1,96,320]{3,2,1,0:T(8,128)(2,1)S(1)} %get-tuple-element.60), channel_id=1, source_target_pairs={{0,8},{8,16},{16,24},{1,9},{9,17},{17,25},{2,10},{10,18},{18,26},{... | collective-permute-start | bytes 184328 | tf_op jit(solution)/shard_map/ppermute | solution.py:15
  94.8 1.3 collective-permute-start.5
  96.1 14.3 %all-gather.2 = bf16[1,1,320,320]{2,3,1,0:T(8,128)(2,1)S(1)} all-gather(bf16[1,1,320,40]{2,3,1,0:T(8,128)(2,1)S(1)} %copy-done.3), channel_id=4, replica_groups=mesh['rows'=4,'batch'=8] {'batch'}, dimensions={3}, use_global_device_ids=true | all-gather | bytes 230400 | tf_op jit(solution)/shard_map/all_gather | solution.py:71
  110.6 1.0 fusion.155
  111.6 2.2 %fusion.31 = f32[6,96,320]{2,1,0:T(8,128)S(1)} fusion(bf16[1,6,96,320]{3,2,1,0:T(8,128)(2,1)S(1)} %fusion.126, bf16[1,1,96,320]{3,2,1,0:T(8,128)(2,1)S(1)} %collective-permute-done.4, bf16[1,6,96,320]{3,2,1,0:T(8,128)(2,1)S(1)} %get-tuple-element.42, bf16[1,6,96,320]{3,2,1,0:T(8,128)(2,1)} %get-tuple-element.43, ...), kind=kOutput, calls=%fused_computation.58 | convolution fusion | flops 358318080 | bytes 2633728 | tf_op jit(solution)/shard_map/bhwk,kc->bhwc/dot_general | solution.py:59
  113.8 0.8 convolution_add_fusion.5
  114.7 0.8 convert_reduce_fusion.2
  115.9 11.1 %all-reduce.4 = (f32[1,1,1,32,1]{3,4,2,1,0:T(1,128)S(1)}, f32[1,1,1,32,1]{3,4,2,1,0:T(1,128)S(1)}) all-reduce(f32[1,1,1,32,1]{3,4,2,1,0:T(1,128)S(1)} %bitcast.188, f32[1,1,1,32,1]{3,4,2,1,0:T(1,128)S(1)} %bitcast.184), channel_id=1, replica_groups=mesh['rows'=4,'batch'=8] {'rows'}, use_global_device_ids=true, to_apply=%region_23.24 | all-reduce | flops 64 | bytes 512 | tf_op jit(solution)/shard_map/psum | solution.py:29
  127.7 1.9 %collective-permute-start.6 = (bf16[1,1,96,320]{3,2,1,0:T(8,128)(2,1)S(1)}, bf16[1,1,96,320]{3,2,1,0:T(8,128)(2,1)S(1)}, u32[]{:S(2)}, u32[]{:S(2)}) collective-permute-start(bf16[1,1,96,320]{3,2,1,0:T(8,128)(2,1)S(1)} %get-tuple-element.58), channel_id=1, source_target_pairs={{0,8},{8,16},{16,24},{1,9},{9,17},{17,25},{2,10},{10,18},{18,26},{... | collective-permute-start | bytes 184328 | tf_op jit(solution)/shard_map/ppermute | solution.py:15
  129.6 1.3 collective-permute-start.7
  131.6 4.3 %collective-permute-done.7 = bf16[1,1,96,320]{3,2,1,0:T(8,128)(2,1)S(1)} collective-permute-done((bf16[1,1,96,320]{3,2,1,0:T(8,128)(2,1)S(1)}, bf16[1,1,96,320]{3,2,1,0:T(8,128)(2,1)S(1)}, u32[]{:S(2)}, u32[]{:S(2)}) %collective-permute-start.7) | collective-permute-done | bytes 61472 | tf_op jit(solution)/shard_map/ppermute | solution.py:18
  136.7 1.0 fusion.154
  137.7 2.0 %fusion.20 = f32[6,96,320]{2,1,0:T(8,128)S(1)} fusion(bf16[1,6,96,320]{3,2,1,0:T(8,128)(2,1)S(1)} %fusion.135, bf16[1,1,96,320]{3,2,1,0:T(8,128)(2,1)} %copy-done.12, bf16[1,6,96,320]{3,2,1,0:T(8,128)(2,1)S(1)} %get-tuple-element.36, bf16[1,6,96,320]{3,2,1,0:T(8,128)(2,1)} %get-tuple-element.37, bf16[1,1,3,960,320]{3,4,2,1,0:T(8,128)(2,1)} %all-gather.17.cloned.1.call-done), kind=kOutput, calls=%fused_computation.47 | convolution fusion | flops 358318080 | bytes 2646016 | tf_op jit(solution)/shard_map/bhwk,kc->bhwc/dot_general | solution.py:59
  139.8 2.8 %convolution_add_fusion.3 = f32[6,96,320]{2,1,0:T(8,128)} fusion(f32[6,96,320]{2,1,0:T(8,128)S(1)} %fusion.20, bf16[1,6,96,320]{3,2,1,0:T(8,128)(2,1)S(1)} %get-tuple-element.34, bf16[1,6,96,320]{3,2,1,0:T(8,128)(2,1)S(1)} %fusion.135, bf16[1,6,96,320]{3,2,1,0:T(8,128)(2,1)S(1)} %get-tuple-element.35, ...), kind=kOutput, calls=%fused_computation.20 | convolution fusion | flops 357396480 | bytes 3235840 | tf_op jit(solution)/shard_map/bhwk,kc->bhwc/dot_general | solution.py:59
  142.7 2.5 %fusion.9 = bf16[1,1,6,96,320]{4,3,2,1,0:T(8,128)(2,1)S(1)} fusion(f32[6,96,320]{2,1,0:T(8,128)} %convolution_add_fusion.3, bf16[1,6,96,320]{3,2,1,0:T(8,128)(2,1)S(1)} %get-tuple-element.76, bf16[1,1,96,320]{3,2,1,0:T(8,128)(2,1)S(1)} %copy-done.10, bf16[1,6,96,320]{3,2,1,0:T(8,128)(2,1)S(1)} %fusion.135, ...), kind=kOutput, calls=%fused_computation.35 | convolution fusion | flops 477573120 | bytes 4091904 | tf_op jit(solution)/shard_map/bhwk,kc->bhwc/dot_general | solution.py:59
  145.2 1.1 pad_maximum_fusion.8
  (114 shorter events, 13.7 us)
Async XLA Ops:
  6.5 3.9 %copy-start = (bf16[1,6,96,320]{3,2,1,0:T(8,128)(2,1)S(1)}, bf16[1,6,96,320]{3,2,1,0:T(8,128)(2,1)}, u32[]{:S(2)}) copy-start(bf16[1,6,96,320]{3,2,1,0:T(8,128)(2,1)} %param.6) | copy-start | bytes 1105924
  6.5 16.3 %copy-start.17 = (f32[2,2,320]{2,1,0:T(2,128)S(1)}, f32[2,2,320]{2,1,0:T(2,128)}, u32[]{:S(2)}) copy-start(f32[2,2,320]{2,1,0:T(2,128)} %param.8) | copy-start | bytes 15364
  6.5 16.3 %copy-start.16 = (f32[2,2,320]{2,1,0:T(2,128)S(1)}, f32[2,2,320]{2,1,0:T(2,128)}, u32[]{:S(2)}) copy-start(f32[2,2,320]{2,1,0:T(2,128)} %param.9) | copy-start | bytes 15364
  6.5 20.8 %copy-start.13 = (bf16[2,1,320,40]{2,3,1,0:T(8,128)(2,1)S(1)}, bf16[2,1,320,40]{2,3,1,0:T(8,128)(2,1)}, u32[]{:S(2)}) copy-start(bf16[2,1,320,40]{2,3,1,0:T(8,128)(2,1)} %param.11) | copy-start | bytes 153604
  6.5 33.3 %all-gather.11.cloned.1.call-start = ((), (), s32[]{:S(2)}) async-start(), calls=%async_computation | async-start | bytes 2211840 | tf_op jit(solution)/shard_map/all_gather | solution.py:71
  8.9 66.5 %all-gather.13.cloned.1.call-start = ((), (), s32[]{:S(2)}) async-start(), calls=%async_computation.1 | async-start | bytes 2211840 | tf_op jit(solution)/shard_map/all_gather | solution.py:71
  9.7 102.0 %all-gather.15.cloned.1.call-start = ((), (), s32[]{:S(2)}) async-start(), calls=%async_computation.2 | async-start | bytes 2211840 | tf_op jit(solution)/shard_map/all_gather | solution.py:71
  10.4 127.3 %all-gather.17.cloned.1.call-start = ((), (), s32[]{:S(2)}) async-start(), calls=%async_computation.3 | async-start | bytes 2211840 | tf_op jit(solution)/shard_map/all_gather | solution.py:71
  23.8 4.1 %collective-permute-start = (bf16[1,1,96,320]{3,2,1,0:T(8,128)(2,1)S(1)}, bf16[1,1,96,320]{3,2,1,0:T(8,128)(2,1)}, u32[]{:S(2)}, u32[]{:S(2)}) collective-permute-start(bf16[1,1,96,320]{3,2,1,0:T(8,128)(2,1)S(1)} %get-tuple-element.64), channel_id=1, source_target_pairs={{0,8},{8,16},{16,24},{1,9},{9,17},{17,25},{2,10},{10,18},{18,26},{... | collective-permute-start | bytes 184328 | tf_op jit(solution)/shard_map/ppermute | solution.py:15
  26.0 6.2 %collective-permute-start.1 = (bf16[1,1,96,320]{3,2,1,0:T(8,128)(2,1)S(1)}, bf16[1,1,96,320]{3,2,1,0:T(8,128)(2,1)S(1)}, u32[]{:S(2)}, u32[]{:S(2)}) collective-permute-start(bf16[1,1,96,320]{3,2,1,0:T(8,128)(2,1)S(1)} %get-tuple-element.63), channel_id=1, source_target_pairs={{8,0},{16,8},{24,16},{9,1},{17,9},{25,17},{10,2},{18,10},{26,18},{... | collective-permute-start | bytes 184328 | tf_op jit(solution)/shard_map/ppermute | solution.py:18
  32.2 0.6 copy-start.5
  39.9 2.1 %copy-start.20 = (bf16[1,1,3,960,320]{3,4,2,1,0:T(8,128)(2,1)S(1)}, bf16[1,1,3,960,320]{3,4,2,1,0:T(8,128)(2,1)}, u32[]{:S(2)}) copy-start(bf16[1,1,3,960,320]{3,4,2,1,0:T(8,128)(2,1)} %all-gather.11.cloned.1.call-done) | copy-start | bytes 5529604
  41.9 0.9 copy-start.6
  42.8 11.5 %copy-start.14 = (f32[320]{0:T(512)S(1)}, f32[320]{0:T(512)}, u32[]{:S(2)}) copy-start(f32[320]{0:T(512)} %get-tuple-element.18) | copy-start | bytes 3844
  42.8 11.5 %copy-start.15 = (f32[320]{0:T(512)S(1)}, f32[320]{0:T(512)}, u32[]{:S(2)}) copy-start(f32[320]{0:T(512)} %get-tuple-element.80) | copy-start | bytes 3844
  42.8 14.9 %copy-start.4 = (bf16[1,1,320,40]{2,3,1,0:T(8,128)(2,1)S(1)}, bf16[1,1,320,40]{2,3,1,0:T(8,128)(2,1)}, u32[]{:S(2)}) copy-start(bf16[1,1,320,40]{2,3,1,0:T(8,128)(2,1)} %get-tuple-element.66) | copy-start | bytes 76804
  54.7 19.0 %collective-permute-start.2 = (bf16[1,1,96,320]{3,2,1,0:T(8,128)(2,1)S(1)}, bf16[1,1,96,320]{3,2,1,0:T(8,128)(2,1)S(1)}, u32[]{:S(2)}, u32[]{:S(2)}) collective-permute-start(bf16[1,1,96,320]{3,2,1,0:T(8,128)(2,1)S(1)} %get-tuple-element.62), channel_id=1, source_target_pairs={{0,8},{8,16},{16,24},{1,9},{9,17},{17,25},{2,10},{10,18},{18,26},{... | collective-permute-start | bytes 184328 | tf_op jit(solution)/shard_map/ppermute | solution.py:15
  56.4 17.3 %collective-permute-start.3 = (bf16[1,1,96,320]{3,2,1,0:T(8,128)(2,1)S(1)}, bf16[1,1,96,320]{3,2,1,0:T(8,128)(2,1)S(1)}, u32[]{:S(2)}, u32[]{:S(2)}) collective-permute-start(bf16[1,1,96,320]{3,2,1,0:T(8,128)(2,1)S(1)} %get-tuple-element.61), channel_id=1, source_target_pairs={{8,0},{16,8},{24,16},{9,1},{17,9},{25,17},{10,2},{18,10},{26,18},{... | collective-permute-start | bytes 184328 | tf_op jit(solution)/shard_map/ppermute | solution.py:18
  74.3 0.6 copy-start.7
  75.4 2.1 %copy-start.19 = (bf16[1,1,3,960,320]{3,4,2,1,0:T(8,128)(2,1)S(1)}, bf16[1,1,3,960,320]{3,4,2,1,0:T(8,128)(2,1)}, u32[]{:S(2)}) copy-start(bf16[1,1,3,960,320]{3,4,2,1,0:T(8,128)(2,1)} %all-gather.13.cloned.1.call-done) | copy-start | bytes 5529604
  77.5 0.9 copy-start.8
  78.4 17.7 %copy-start.3 = (bf16[1,1,320,40]{2,3,1,0:T(8,128)(2,1)S(1)}, bf16[1,1,320,40]{2,3,1,0:T(8,128)(2,1)}, u32[]{:S(2)}) copy-start(bf16[1,1,320,40]{2,3,1,0:T(8,128)(2,1)} %get-tuple-element.65) | copy-start | bytes 76804
  91.4 19.0 %collective-permute-start.4 = (bf16[1,1,96,320]{3,2,1,0:T(8,128)(2,1)S(1)}, bf16[1,1,96,320]{3,2,1,0:T(8,128)(2,1)S(1)}, u32[]{:S(2)}, u32[]{:S(2)}) collective-permute-start(bf16[1,1,96,320]{3,2,1,0:T(8,128)(2,1)S(1)} %get-tuple-element.60), channel_id=1, source_target_pairs={{0,8},{8,16},{16,24},{1,9},{9,17},{17,25},{2,10},{10,18},{18,26},{... | collective-permute-start | bytes 184328 | tf_op jit(solution)/shard_map/ppermute | solution.py:15
  94.8 15.7 %collective-permute-start.5 = (bf16[1,1,96,320]{3,2,1,0:T(8,128)(2,1)S(1)}, bf16[1,1,96,320]{3,2,1,0:T(8,128)(2,1)S(1)}, u32[]{:S(2)}, u32[]{:S(2)}) collective-permute-start(bf16[1,1,96,320]{3,2,1,0:T(8,128)(2,1)S(1)} %get-tuple-element.59), channel_id=1, source_target_pairs={{8,0},{16,8},{24,16},{9,1},{17,9},{25,17},{10,2},{18,10},{26,18},{... | collective-permute-start | bytes 184328 | tf_op jit(solution)/shard_map/ppermute | solution.py:18
  111.6 2.2 %copy-start.18 = (bf16[1,1,3,960,320]{3,4,2,1,0:T(8,128)(2,1)S(1)}, bf16[1,1,3,960,320]{3,4,2,1,0:T(8,128)(2,1)}, u32[]{:S(2)}) copy-start(bf16[1,1,3,960,320]{3,4,2,1,0:T(8,128)(2,1)} %all-gather.15.cloned.1.call-done) | copy-start | bytes 5529604
  114.6 16.3 %copy-start.2 = (bf16[2,1,6,96,320]{4,3,2,1,0:T(8,128)(2,1)S(1)}, bf16[2,1,6,96,320]{4,3,2,1,0:T(8,128)(2,1)}, u32[]{:S(2)}) copy-start(bf16[2,1,6,96,320]{4,3,2,1,0:T(8,128)(2,1)} %param.7) | copy-start | bytes 2211844
  127.7 3.8 %collective-permute-start.6 = (bf16[1,1,96,320]{3,2,1,0:T(8,128)(2,1)S(1)}, bf16[1,1,96,320]{3,2,1,0:T(8,128)(2,1)S(1)}, u32[]{:S(2)}, u32[]{:S(2)}) collective-permute-start(bf16[1,1,96,320]{3,2,1,0:T(8,128)(2,1)S(1)} %get-tuple-element.58), channel_id=1, source_target_pairs={{0,8},{8,16},{16,24},{1,9},{9,17},{17,25},{2,10},{10,18},{18,26},{... | collective-permute-start | bytes 184328 | tf_op jit(solution)/shard_map/ppermute | solution.py:15
  129.6 6.3 %collective-permute-start.7 = (bf16[1,1,96,320]{3,2,1,0:T(8,128)(2,1)S(1)}, bf16[1,1,96,320]{3,2,1,0:T(8,128)(2,1)S(1)}, u32[]{:S(2)}, u32[]{:S(2)}) collective-permute-start(bf16[1,1,96,320]{3,2,1,0:T(8,128)(2,1)S(1)} %get-tuple-element.57), channel_id=1, source_target_pairs={{8,0},{16,8},{24,16},{9,1},{17,9},{25,17},{10,2},{18,10},{26,18},{... | collective-permute-start | bytes 184328 | tf_op jit(solution)/shard_map/ppermute | solution.py:18
  131.6 4.3 %copy-start.12 = (bf16[1,1,96,320]{3,2,1,0:T(8,128)(2,1)}, bf16[1,1,96,320]{3,2,1,0:T(8,128)(2,1)S(1)}, u32[]{:S(2)}) copy-start(bf16[1,1,96,320]{3,2,1,0:T(8,128)(2,1)S(1)} %collective-permute-done.6) | copy-start | bytes 184324
  135.9 0.6 copy-start.9
  139.8 2.9 %copy-start.1 = (bf16[1,1,320,320]{2,3,1,0:T(8,128)(2,1)S(1)}, bf16[1,1,320,320]{2,3,1,0:T(8,128)(2,1)}, u32[]{:S(2)}) copy-start(bf16[1,1,320,320]{2,3,1,0:T(8,128)(2,1)} %all-gather.5) | copy-start | bytes 614404
  139.8 2.9 %copy-start.10 = (bf16[1,1,96,320]{3,2,1,0:T(8,128)(2,1)S(1)}, bf16[1,1,96,320]{3,2,1,0:T(8,128)(2,1)}, u32[]{:S(2)}) copy-start(bf16[1,1,96,320]{3,2,1,0:T(8,128)(2,1)} %copy-done.9) | copy-start | bytes 184324
  (1 other events, 0.6 us)
Sparse Core Ops, SparseCore 0:
  9.0 30.7 all-gather.10
  41.5 29.1 all-gather.12
  72.2 27.3 all-gather.14
  101.1 27.4 all-gather.16
where the time goes:
time: 154 us; the launch traced here: 153 us
  blocking collectives  73.5 us (48%)
  matrix products  19.1 us (12%)
  waiting for transfers between devices  15.9 us (10%)
  starting transfers between devices  14.4 us (9%)
  between operations  13.6 us (9%)
  local copies, waits for them, and re-layouts  11.2 us (7%)
  other arithmetic  5.14 us (3%)
    psum x4, blocking collectives, normalize(): lax.psum((jnp.sum(grouped, axis=(1, 2, 4), keepdims=True), jnp.sum(groupe...  43.2 us
    all_gather x2, blocking collectives, convolve(): complete = lax.all_gather(weight, 'batch', axis=2, tiled=True)  30.3 us
    dot_general x13, matrix products, apply_taps(): jnp.einsum('bhwk,kc->bhwc', stacked, weight_piece[row_tap], preferred_ele...  19.1 us
    ppermute x4, starting transfers between devices, extended(): lax.ppermute(lax.slice_in_dim(block, block.shape[dim] - width, None, axis...  9.07 us
    ppermute x4, waiting for transfers between devices, extended(): lax.ppermute(lax.slice_in_dim(block, 0, width, axis=dim), axis, backward)  8.61 us
    all_gather x4, waiting for transfers between devices, convolve(): complete = lax.all_gather(weight, 'batch', axis=2, tiled=True)  5.62 us
    ppermute x4, starting transfers between devices, extended(): lax.ppermute(lax.slice_in_dim(block, 0, width, axis=dim), axis, backward)  5.16 us
  transfers between devices with their start and end apart: 12, of which 4 were waited for; matrix products, arithmetic and copies ran while one was open for 14% of the time, Pallas kernels for 0%

commit v1 on v0

--- a/solution.py
+++ b/solution.py
@@ -68,7 +68,8 @@
         padded = jnp.pad(padded, ((0, 0), (0, 0), (1, 1), (0, 0)))
     else:
         padded = values
-    complete = lax.all_gather(weight, "batch", axis=2, tiled=True)
+    _fill_slots = lambda my_tile: jnp.concatenate(lax.all_gather(my_tile, "batch"), axis=2)
+    complete = _fill_slots(weight)
     return apply_taps(padded, complete)
 
 

time: 154 us -> 172 us (1.12)
  waiting for transfers between devices: 15.9 us -> 28.3 us
  local copies, waits for them, and re-layouts: 11.2 us -> 23.5 us
  matrix products: 19.1 us -> 14.4 us
    all_gather x4, waiting for transfers between devices: 5.62 us -> 23.1 us  [convolve(): lax.all_gather(my_tile, 'batch')]
    slice x1 -> x5, local copies, waits for them, and re-layouts: 2.3 us -> 12.3 us  [the longest x4 9.91 us: apply_taps(): weight_piece[row_tap]]
    ppermute x4, waiting for transfers between devices: 8.61 us -> 3.84 us  [extended(): lax.ppermute(lax.slice_in_dim(block, 0, width, axis=dim), axis, backward)]
    dot_general x13, matrix products: 19.1 us -> 14.4 us  [apply_taps(): jnp.einsum('bhwk,kc->bhwc', stacked, weight_piece[row_tap], preferred_ele...]
    unnamed x42 -> x38, local copies, waits for them, and re-layouts: 2.68 us -> 4.7 us
  transfers between devices with their start and end apart: 12 -> 12, of which waited for: 4 -> 3; matrix products, arithmetic and copies ran while one was open for 14% -> 14% of each run, Pallas kernels for 0% -> 0%
where the time goes in v1:
time: 172 us; the launch traced here: 171 us
  blocking collectives  73.6 us (43%)
  waiting for transfers between devices  28.3 us (16%)
  local copies, waits for them, and re-layouts  23.5 us (14%)
  matrix products  14.4 us (8%)
  between operations  13.6 us (8%)
  starting transfers between devices  13.4 us (8%)
  other arithmetic  4.24 us (2%)
    psum x4, blocking collectives, normalize(): lax.psum((jnp.sum(grouped, axis=(1, 2, 4), keepdims=True), jnp.sum(groupe...  42.2 us
    all_gather x2, blocking collectives, convolve(): lax.all_gather(my_tile, 'batch')  31.3 us
    all_gather x4, waiting for transfers between devices, convolve(): lax.all_gather(my_tile, 'batch')  23.1 us
    dot_general x13, matrix products, apply_taps(): jnp.einsum('bhwk,kc->bhwc', stacked, weight_piece[row_tap], preferred_ele...  14.4 us
    slice x4, local copies, waits for them, and re-layouts, apply_taps(): weight_piece[row_tap]  9.91 us
    ppermute x4, starting transfers between devices, extended(): lax.ppermute(lax.slice_in_dim(block, block.shape[dim] - width, None, axis...  7.96 us
    ppermute x4, starting transfers between devices, extended(): lax.ppermute(lax.slice_in_dim(block, 0, width, axis=dim), axis, backward)  5.35 us
    unnamed x38, local copies, waits for them, and re-layouts  4.7 us
  transfers between devices with their start and end apart: 12, of which 3 were waited for; matrix products, arithmetic and copies ran while one was open for 14% of the time, Pallas kernels for 0%

profile of v1, /device:TPU:0, one launch (start us, length us, event | category | flops | bytes accessed | tf_op | source)
XLA Modules:
  0.0 171.1 jit_solution(10728988175701597753)
XLA Ops:
  6.5 2.4 %fusion.155 = (bf16[1,1,3,960,40]{3,4,2,1,0:T(8,128)(2,1)}, bf16[1,1,3,960,40]{3,4,2,1,0:T(8,128)(2,1)}, bf16[1,1,3,960,40]{3,4,2,1,0:T(8,128)(2,1)}, bf16[1,1,3,960,40]{3,4,2,1,0:T(8,128)(2,1)}) fusion(bf16[2,2,3,960,40]{3,4,2,1,0:T(8,128)(2,1)} %param.10), kind=kLoop, calls=%fused_computation.205 | loop fusion | bytes 1843200 | tf_op jit(solution)/shard_map/slice | solution.py:81
  11.1 11.4 %all-reduce.7 = (f32[1,1,1,32,1]{3,4,2,1,0:T(1,128)S(1)}, f32[1,1,1,32,1]{3,4,2,1,0:T(1,128)S(1)}) all-reduce(f32[1,1,1,32,1]{3,4,2,1,0:T(1,128)S(1)} %bitcast.204, f32[1,1,1,32,1]{3,4,2,1,0:T(1,128)S(1)} %bitcast.202), channel_id=1, replica_groups=mesh['rows'=4,'batch'=8] {'rows'}, use_global_device_ids=true, to_apply=%region_5.6 | all-reduce | flops 64 | bytes 512 | tf_op jit(solution)/shard_map/psum | solution.py:29
  23.3 1.5 collective-permute-start
  24.9 1.3 collective-permute-start.1
  26.2 16.7 %all_gather.23 = bf16[8,1,320,40]{2,3,1,0:T(8,128)(2,1)} all-gather(bf16[1,1,320,40]{2,3,1,0:T(8,128)(2,1)S(1)} %get-tuple-element.78), channel_id=1, replica_groups=mesh['rows'=4,'batch'=8] {'batch'}, dimensions={0}, use_global_device_ids=true | all-gather | bytes 230400 | tf_op jit(solution)/shard_map/all_gather | solution.py:71
  42.9 14.7 %all_gather.20 = bf16[8,1,320,40]{2,3,1,0:T(8,128)(2,1)S(1)} all-gather(bf16[1,1,320,40]{2,3,1,0:T(8,128)(2,1)S(1)} %get-tuple-element.77), channel_id=1, replica_groups=mesh['rows'=4,'batch'=8] {'batch'}, dimensions={0}, use_global_device_ids=true | all-gather | bytes 230400 | tf_op jit(solution)/shard_map/all_gather | solution.py:71
  57.8 1.0 fusion.159
  58.8 1.7 %fusion.154 = (bf16[1,960,8,40]{1,3,0,2:T(8,128)(2,1)S(1)}, bf16[1,960,8,40]{1,3,0,2:T(8,128)(2,1)S(1)}, bf16[1,960,8,40]{1,3,0,2:T(8,128)(2,1)S(1)}) fusion(bf16[3,960,8,40]{1,3,0,2:T(8,128)(2,1)} %bitcast.184), kind=kLoop, calls=%fused_computation.204 | loop fusion | bytes 3686400 | tf_op jit(solution)/shard_map/slice | solution.py:60
  62.2 0.8 convert_reduce_fusion.3
  63.4 11.2 %all-reduce.6 = (f32[1,1,1,32,1]{3,4,2,1,0:T(1,128)S(1)}, f32[1,1,1,32,1]{3,4,2,1,0:T(1,128)S(1)}) all-reduce(f32[1,1,1,32,1]{3,4,2,1,0:T(1,128)S(1)} %bitcast.205, f32[1,1,1,32,1]{3,4,2,1,0:T(1,128)S(1)} %bitcast.200), channel_id=1, replica_groups=mesh['rows'=4,'batch'=8] {'rows'}, use_global_device_ids=true, to_apply=%region_11.12 | all-reduce | flops 64 | bytes 512 | tf_op jit(solution)/shard_map/psum | solution.py:29
  75.3 3.3 %collective-permute-start.2 = (bf16[1,1,96,320]{3,2,1,0:T(8,128)(2,1)S(1)}, bf16[1,1,96,320]{3,2,1,0:T(8,128)(2,1)S(1)}, u32[]{:S(2)}, u32[]{:S(2)}) collective-permute-start(bf16[1,1,96,320]{3,2,1,0:T(8,128)(2,1)S(1)} %get-tuple-element.74), channel_id=1, source_target_pairs={{0,8},{8,16},{16,24},{1,9},{9,17},{17,25},{2,10},{10,18},{18,26},{... | collective-permute-start | bytes 184328 | tf_op jit(solution)/shard_map/ppermute | solution.py:15
  78.6 1.3 collective-permute-start.3
  80.0 2.9 %fusion.153 = (bf16[1,960,8,40]{1,3,0,2:T(8,128)(2,1)S(1)}, bf16[1,960,8,40]{1,3,0,2:T(8,128)(2,1)}, bf16[1,960,8,40]{1,3,0,2:T(8,128)(2,1)}) fusion(bf16[3,960,8,40]{1,3,0,2:T(8,128)(2,1)} %bitcast.182), kind=kLoop, calls=%fused_computation.203 | loop fusion | bytes 3686400 | tf_op jit(solution)/shard_map/slice | solution.py:60
  82.9 18.0 %all-gather.13.cloned.1.call-done = bf16[8,1,3,960,40]{3,4,2,1,0:T(8,128)(2,1)} async-done(((bf16[1,1,3,960,40]{3,4,2,1,0:T(8,128)(2,1)}), bf16[8,1,3,960,40]{3,4,2,1,0:T(8,128)(2,1)}) %all-gather.13.cloned.1.call-update) | async-done | bytes 1843216 | tf_op jit(solution)/shard_map/all_gather | solution.py:71
  100.8 2.5 %fusion.152 = (bf16[1,960,8,40]{1,3,0,2:T(8,128)(2,1)S(1)}, bf16[1,960,8,40]{1,3,0,2:T(8,128)(2,1)S(1)}, bf16[1,960,8,40]{1,3,0,2:T(8,128)(2,1)}) fusion(bf16[3,960,8,40]{1,3,0,2:T(8,128)(2,1)} %bitcast.183), kind=kLoop, calls=%fused_computation.202 | loop fusion | bytes 3686400 | tf_op jit(solution)/shard_map/slice | solution.py:60
  107.0 0.8 convolution_add_fusion.7
  107.9 1.5 convert_reduce_fusion
  111.2 9.8 %all-reduce.5 = (f32[1,1,1,32,1]{3,4,2,1,0:T(1,128)S(1)}, f32[1,1,1,32,1]{3,4,2,1,0:T(1,128)S(1)}) all-reduce(f32[1,1,1,32,1]{3,4,2,1,0:T(1,128)S(1)} %bitcast.206, f32[1,1,1,32,1]{3,4,2,1,0:T(1,128)S(1)} %bitcast.201), channel_id=1, replica_groups=mesh['rows'=4,'batch'=8] {'rows'}, use_global_device_ids=true, to_apply=%region_17.18 | all-reduce | flops 64 | bytes 512 | tf_op jit(solution)/shard_map/psum | solution.py:29
  121.7 1.6 collective-permute-start.4
  123.3 1.5 collective-permute-start.5
  124.8 5.1 %all-gather.15.cloned.1.call-done = bf16[8,1,3,960,40]{3,4,2,1,0:T(8,128)(2,1)} async-done(((bf16[1,1,3,960,40]{3,4,2,1,0:T(8,128)(2,1)}), bf16[8,1,3,960,40]{3,4,2,1,0:T(8,128)(2,1)}) %all-gather.15.cloned.1.call-update) | async-done | bytes 1843216 | tf_op jit(solution)/shard_map/all_gather | solution.py:71
  129.9 2.7 %fusion.151 = (bf16[1,960,8,40]{1,3,0,2:T(8,128)(2,1)S(1)}, bf16[1,960,8,40]{1,3,0,2:T(8,128)(2,1)}, bf16[1,960,8,40]{1,3,0,2:T(8,128)(2,1)}) fusion(bf16[3,960,8,40]{1,3,0,2:T(8,128)(2,1)} %bitcast.181), kind=kLoop, calls=%fused_computation.201 | loop fusion | bytes 3686400 | tf_op jit(solution)/shard_map/slice | solution.py:60
  136.8 0.8 convert_reduce_fusion.2
  138.1 9.8 %all-reduce.4 = (f32[1,1,1,32,1]{3,4,2,1,0:T(1,128)S(1)}, f32[1,1,1,32,1]{3,4,2,1,0:T(1,128)S(1)}) all-reduce(f32[1,1,1,32,1]{3,4,2,1,0:T(1,128)S(1)} %bitcast.203, f32[1,1,1,32,1]{3,4,2,1,0:T(1,128)S(1)} %bitcast.199), channel_id=1, replica_groups=mesh['rows'=4,'batch'=8] {'rows'}, use_global_device_ids=true, to_apply=%region_23.24 | all-reduce | flops 64 | bytes 512 | tf_op jit(solution)/shard_map/psum | solution.py:29
  148.7 1.6 collective-permute-start.6
  150.3 1.3 collective-permute-start.7
  151.6 1.4 fusion.10
  153.0 3.8 %collective-permute-done.7 = bf16[1,1,96,320]{3,2,1,0:T(8,128)(2,1)S(1)} collective-permute-done((bf16[1,1,96,320]{3,2,1,0:T(8,128)(2,1)S(1)}, bf16[1,1,96,320]{3,2,1,0:T(8,128)(2,1)S(1)}, u32[]{:S(2)}, u32[]{:S(2)}) %collective-permute-start.7) | collective-permute-done | bytes 61472 | tf_op jit(solution)/shard_map/ppermute | solution.py:18
  157.1 1.1 fusion.156
  159.3 1.7 %convolution_add_fusion.3 = f32[6,96,320]{2,1,0:T(8,128)} fusion(f32[6,96,320]{2,1,0:T(8,128)S(1)} %fusion.20, bf16[960,320,1]{0,1,2:T(8,128)(2,1)S(1)} %bitcast.190, bf16[1,6,96,320]{3,2,1,0:T(8,128)(2,1)S(1)} %get-tuple-element.46, bf16[1,6,96,320]{3,2,1,0:T(8,128)(2,1)S(1)} %fusion.135, bf16[1,6,96,320]{3,2,1,0:T(8,128)(2,1)S(1)} %get-tuple-element.47), kind=kOutput, calls=%fused_computation.20 | convolution fusion | flops 357396480 | bytes 3194880 | tf_op jit(solution)/shard_map/bhwk,kc->bhwc/dot_general | solution.py:59
  161.0 2.5 %fusion.9 = bf16[1,1,6,96,320]{4,3,2,1,0:T(8,128)(2,1)S(1)} fusion(bf16[320,320,1]{0,1,2:T(8,128)(2,1)S(1)} %bitcast.198, f32[6,96,320]{2,1,0:T(8,128)} %convolution_add_fusion.3, bf16[960,320,1]{0,1,2:T(8,128)(2,1)S(1)} %bitcast.187, bf16[1,6,96,320]{3,2,1,0:T(8,128)(2,1)S(1)} %get-tuple-element.88, ...), kind=kOutput, calls=%fused_computation.35 | convolution fusion | flops 477573120 | bytes 3829760 | tf_op jit(solution)/shard_map/bhwk,kc->bhwc/dot_general | solution.py:59
  163.5 1.1 pad_maximum_fusion.8
  (114 shorter events, 18.6 us)
Async XLA Ops:
  6.5 4.0 %copy-start = (bf16[1,6,96,320]{3,2,1,0:T(8,128)(2,1)S(1)}, bf16[1,6,96,320]{3,2,1,0:T(8,128)(2,1)}, u32[]{:S(2)}) copy-start(bf16[1,6,96,320]{3,2,1,0:T(8,128)(2,1)} %param.6) | copy-start | bytes 1105924
  6.5 16.4 %copy-start.18 = (f32[2,2,320]{2,1,0:T(2,128)S(1)}, f32[2,2,320]{2,1,0:T(2,128)}, u32[]{:S(2)}) copy-start(f32[2,2,320]{2,1,0:T(2,128)} %param.8) | copy-start | bytes 15364
  6.5 16.4 %copy-start.17 = (f32[2,2,320]{2,1,0:T(2,128)S(1)}, f32[2,2,320]{2,1,0:T(2,128)}, u32[]{:S(2)}) copy-start(f32[2,2,320]{2,1,0:T(2,128)} %param.9) | copy-start | bytes 15364
  6.5 52.2 %all-gather.9.cloned.1.call-start = ((), (), s32[]{:S(2)}) async-start(), calls=%async_computation | async-start | bytes 2211840 | tf_op jit(solution)/shard_map/all_gather | solution.py:71
  9.0 71.0 %all-gather.11.cloned.1.call-start = ((), (), s32[]{:S(2)}) async-start(), calls=%async_computation.1 | async-start | bytes 2211840 | tf_op jit(solution)/shard_map/all_gather | solution.py:71
  9.0 17.2 %copy-start.16 = (bf16[2,1,320,40]{2,3,1,0:T(8,128)(2,1)S(1)}, bf16[2,1,320,40]{2,3,1,0:T(8,128)(2,1)}, u32[]{:S(2)}) copy-start(bf16[2,1,320,40]{2,3,1,0:T(8,128)(2,1)} %param.11) | copy-start | bytes 153604
  9.7 91.1 %all-gather.13.cloned.1.call-start = ((), (), s32[]{:S(2)}) async-start(), calls=%async_computation.2 | async-start | bytes 2211840 | tf_op jit(solution)/shard_map/all_gather | solution.py:71
  10.5 119.4 %all-gather.15.cloned.1.call-start = ((), (), s32[]{:S(2)}) async-start(), calls=%async_computation.3 | async-start | bytes 2211840 | tf_op jit(solution)/shard_map/all_gather | solution.py:71
  23.3 34.2 %collective-permute-start = (bf16[1,1,96,320]{3,2,1,0:T(8,128)(2,1)S(1)}, bf16[1,1,96,320]{3,2,1,0:T(8,128)(2,1)S(1)}, u32[]{:S(2)}, u32[]{:S(2)}) collective-permute-start(bf16[1,1,96,320]{3,2,1,0:T(8,128)(2,1)S(1)} %get-tuple-element.76), channel_id=1, source_target_pairs={{0,8},{8,16},{16,24},{1,9},{9,17},{17,25},{2,10},{10,18},{18,26},{... | collective-permute-start | bytes 184328 | tf_op jit(solution)/shard_map/ppermute | solution.py:15
  24.9 32.7 %collective-permute-start.1 = (bf16[1,1,96,320]{3,2,1,0:T(8,128)(2,1)S(1)}, bf16[1,1,96,320]{3,2,1,0:T(8,128)(2,1)S(1)}, u32[]{:S(2)}, u32[]{:S(2)}) collective-permute-start(bf16[1,1,96,320]{3,2,1,0:T(8,128)(2,1)S(1)} %get-tuple-element.75), channel_id=1, source_target_pairs={{8,0},{16,8},{24,16},{9,1},{17,9},{25,17},{10,2},{18,10},{26,18},{... | collective-permute-start | bytes 184328 | tf_op jit(solution)/shard_map/ppermute | solution.py:18
  58.8 1.8 %copy-start.6 = (bf16[1,6,96,320]{3,2,1,0:T(8,128)(2,1)S(1)}, bf16[1,6,96,320]{3,2,1,0:T(8,128)(2,1)}, u32[]{:S(2)}) copy-start(bf16[1,6,96,320]{3,2,1,0:T(8,128)(2,1)} %get-tuple-element.67) | copy-start | bytes 1105924
  75.3 28.0 %collective-permute-start.2 = (bf16[1,1,96,320]{3,2,1,0:T(8,128)(2,1)S(1)}, bf16[1,1,96,320]{3,2,1,0:T(8,128)(2,1)S(1)}, u32[]{:S(2)}, u32[]{:S(2)}) collective-permute-start(bf16[1,1,96,320]{3,2,1,0:T(8,128)(2,1)S(1)} %get-tuple-element.74), channel_id=1, source_target_pairs={{0,8},{8,16},{16,24},{1,9},{9,17},{17,25},{2,10},{10,18},{18,26},{... | collective-permute-start | bytes 184328 | tf_op jit(solution)/shard_map/ppermute | solution.py:15
  78.6 24.7 %collective-permute-start.3 = (bf16[1,1,96,320]{3,2,1,0:T(8,128)(2,1)S(1)}, bf16[1,1,96,320]{3,2,1,0:T(8,128)(2,1)S(1)}, u32[]{:S(2)}, u32[]{:S(2)}) collective-permute-start(bf16[1,1,96,320]{3,2,1,0:T(8,128)(2,1)S(1)} %get-tuple-element.73), channel_id=1, source_target_pairs={{8,0},{16,8},{24,16},{9,1},{17,9},{25,17},{10,2},{18,10},{26,18},{... | collective-permute-start | bytes 184328 | tf_op jit(solution)/shard_map/ppermute | solution.py:18
  103.4 0.6 copy-start.12
  104.0 0.6 copy-start.8
  104.8 1.1 copy-start.5
  104.8 1.1 copy-start.13
  105.9 1.1 copy-start.4
  107.0 0.9 copy-start.9
  121.7 10.9 %collective-permute-start.4 = (bf16[1,1,96,320]{3,2,1,0:T(8,128)(2,1)S(1)}, bf16[1,1,96,320]{3,2,1,0:T(8,128)(2,1)S(1)}, u32[]{:S(2)}, u32[]{:S(2)}) collective-permute-start(bf16[1,1,96,320]{3,2,1,0:T(8,128)(2,1)S(1)} %get-tuple-element.72), channel_id=1, source_target_pairs={{0,8},{8,16},{16,24},{1,9},{9,17},{17,25},{2,10},{10,18},{18,26},{... | collective-permute-start | bytes 184328 | tf_op jit(solution)/shard_map/ppermute | solution.py:15
  123.3 9.3 %collective-permute-start.5 = (bf16[1,1,96,320]{3,2,1,0:T(8,128)(2,1)S(1)}, bf16[1,1,96,320]{3,2,1,0:T(8,128)(2,1)S(1)}, u32[]{:S(2)}, u32[]{:S(2)}) collective-permute-start(bf16[1,1,96,320]{3,2,1,0:T(8,128)(2,1)S(1)} %get-tuple-element.71), channel_id=1, source_target_pairs={{8,0},{16,8},{24,16},{9,1},{17,9},{25,17},{10,2},{18,10},{26,18},{... | collective-permute-start | bytes 184328 | tf_op jit(solution)/shard_map/ppermute | solution.py:18
  132.6 0.6 copy-start.14
  133.2 0.6 copy-start.10
  134.1 1.1 copy-start.1
  134.1 1.1 copy-start.15
  136.0 0.9 copy-start.11
  148.7 4.3 %collective-permute-start.6 = (bf16[1,1,96,320]{3,2,1,0:T(8,128)(2,1)S(1)}, bf16[1,1,96,320]{3,2,1,0:T(8,128)(2,1)S(1)}, u32[]{:S(2)}, u32[]{:S(2)}) collective-permute-start(bf16[1,1,96,320]{3,2,1,0:T(8,128)(2,1)S(1)} %get-tuple-element.70), channel_id=1, source_target_pairs={{0,8},{8,16},{16,24},{1,9},{9,17},{17,25},{2,10},{10,18},{18,26},{... | collective-permute-start | bytes 184328 | tf_op jit(solution)/shard_map/ppermute | solution.py:15
  150.3 6.6 %collective-permute-start.7 = (bf16[1,1,96,320]{3,2,1,0:T(8,128)(2,1)S(1)}, bf16[1,1,96,320]{3,2,1,0:T(8,128)(2,1)S(1)}, u32[]{:S(2)}, u32[]{:S(2)}) collective-permute-start(bf16[1,1,96,320]{3,2,1,0:T(8,128)(2,1)S(1)} %get-tuple-element.69), channel_id=1, source_target_pairs={{8,0},{16,8},{24,16},{9,1},{17,9},{25,17},{10,2},{18,10},{26,18},{... | collective-permute-start | bytes 184328 | tf_op jit(solution)/shard_map/ppermute | solution.py:18
  157.1 1.1 copy-start.3
  158.2 1.1 copy-start.2
  159.3 1.7 %copy-start.7 = (bf16[8,1,320,40]{2,3,1,0:T(8,128)(2,1)S(1)}, bf16[8,1,320,40]{2,3,1,0:T(8,128)(2,1)}, u32[]{:S(2)}) copy-start(bf16[8,1,320,40]{2,3,1,0:T(8,128)(2,1)} %all_gather.23) | copy-start | bytes 614404
Sparse Core Ops, SparseCore 0:
  9.1 32.4 all-gather.8
  43.2 28.4 all-gather.10
  73.3 27.4 all-gather.12
  102.3 27.4 all-gather.14
